TPU v7x, 32 devices: a whole 2x2x4 slice. The times are simulated.
32 devices in a mesh: pgroup: 8 (over y, x, core), tile: 4 (over z).
Axes of the slice: x: 2, y: 2, z: 4, core: 2. Of those that a mesh axis runs over, the one named last changes fastest.
Arguments:
- images: float32 [64, 256, 2048], P(('pgroup', 'tile')), may hold values from -6 to 6
- beams: float32 [64, 256, 2048], P(('pgroup', 'tile')), may hold values from 0.2 to 1
- row_block: int32 [64], P(('pgroup', 'tile')), may hold values from 0 to 14, as said below
- col_block: int32 [64], P(('pgroup', 'tile')), may hold values from 0 to 16
- band: int32 [64, 2], P(('pgroup', 'tile')), may hold values from 0 to 3
- row_frac: float32 [64], P(('pgroup', 'tile')), may hold values from 0.05 to 0.95
- col_frac: float32 [64], P(('pgroup', 'tile')), may hold values from 0.05 to 0.95
Outputs:
- numer: float32 [2048, 4096], P('tile', 'pgroup')
- weight: float32 [2048, 4096], P('tile', 'pgroup')
- normalised: float32 [2048, 4096], P('tile', 'pgroup')
Inputs may be any that keep to these rules, and one draw needn't show every extreme that they name: With t = (p // 2) mod 4, row_block[p] - 4 t lies in 0 to 2, and the largest value is taken in every draw.
All inputs are finite; a program needn't handle non-finite values.
Results may differ from a plain program's by a relative error of at most 0.00002.
Values sent between devices are 32-bit elements; how exact they have to be, the bound alone decides.
A program may use at most 128 MiB of HBM per device.

v0:
```python
import jax
import jax.numpy as jnp
from jax import lax
from jax.sharding import PartitionSpec as P

IMG_BLOCKS = 2
TILE_BLOCKS = 4
SKY_COLS = 4096
HALO = 4


def shifted(block, axis, distance):
    devices = range(lax.axis_size(axis))
    route = [(i - distance, i) for i in devices if i - distance in devices]
    return lax.ppermute(block, axis, route)


def contribution(image_block, beam_block, shift, row_f, col_f, margin):
    stacked = jnp.stack([beam_block * image_block, beam_block * beam_block])
    moved = jnp.concatenate([jnp.zeros_like(stacked[:, :, :1]), stacked[:, :, :-1]], axis=2)
    banded = (1.0 - col_f) * stacked + col_f * moved
    empty = jnp.zeros((2, 128 + margin, banded.shape[2]), jnp.float32)
    zero = jnp.int32(0)
    first = lax.dynamic_update_slice(empty, (1.0 - row_f) * banded, (zero, shift, zero))
    second = lax.dynamic_update_slice(empty, row_f * banded, (zero, shift + 1, zero))
    return first + second


def body(images, beams, row_block, col_block, band, row_frac, col_frac):
    own_rows = TILE_BLOCKS * 128
    canvas = jnp.zeros((2, own_rows + HALO, SKY_COLS), jnp.float32)
    first_block = lax.axis_index("tile") * TILE_BLOCKS
    zero = jnp.int32(0)
    for which in range(images.shape[0]):
        for block in range(IMG_BLOCKS):
            piece = contribution(
                images[which, block * 128 : (block + 1) * 128],
                beams[which, block * 128 : (block + 1) * 128],
                band[which, block],
                row_frac[which],
                col_frac[which],
                HALO,
            )
            row_start = (row_block[which] - first_block + block) * 128
            col_start = col_block[which] * 128
            old = lax.dynamic_slice(canvas, (zero, row_start, col_start), piece.shape)
            canvas = lax.dynamic_update_slice(canvas, old + piece, (zero, row_start, col_start))
    border = shifted(canvas[:, own_rows:], "tile", 1)
    owned = canvas[:, :own_rows].at[:, :HALO].add(border)
    summed = lax.psum_scatter(owned, "pgroup", scatter_dimension=2, tiled=True)
    numer = summed[0]
    weight = summed[1]
    normalised = numer / jnp.maximum(weight, 0.05)
    return (numer, weight, normalised)


def solution(mesh):
    return jax.shard_map(
        body,
        mesh=mesh,
        in_specs=(
            P(("pgroup", "tile"), None, None),
            P(("pgroup", "tile"), None, None),
            P(("pgroup", "tile")),
            P(("pgroup", "tile")),
            P(("pgroup", "tile"), None),
            P(("pgroup", "tile")),
            P(("pgroup", "tile")),
        ),
        out_specs=(P("tile", "pgroup"), P("tile", "pgroup"), P("tile", "pgroup")),
        check_vma=False,
    )
```

profile of v0, /device:TPU:0, one launch (start us, length us, event | category | flops | bytes accessed | tf_op | source)
XLA Modules:
  0.0 347.9 jit_solution(6666681168873235958)
XLA Ops:
  12.5 1.5 fusion.13
  28.9 5.7 %slice_multiply_fusion.4 = (f32[1,128,2048]{2,1,0:T(8,128)}, f32[1,128,2048]{2,1,0:T(8,128)S(1)}, f32[1,128,2048]{2,1,0:T(8,128)S(1)}, f32[1,128,2048]{2,1,0:T(8...) fusion(f32[2,256,2048]{2,1,0:T(8,128)} %param.10, ...), kind=kLoop, calls=%fused_computation.42 | loop fusion | flops 2097152 | bytes 16777216 | tf_op jit(solution)/shard_map/mul | solution.py:19
  37.9 2.7 broadcast_multiply_fusion.3
  41.8 1.7 broadcast.39.clone.1
  43.4 6.7 %dynamic_update_slice.48 = f32[2,132,2048]{2,1,0:T(8,128)} dynamic-update-slice(f32[2,132,2048]{2,1,0:T(8,128)} %broadcast.39.clone.1, f32[2,128,2048]{2,1,0:T(8,128)S(1)} %broadcast_multiply_fusion.2, s32[]{:T(128)} %constant.49.clone.1, s32[]{:T(128)S(6)} %select_n.55, s32[]{:T(128)} %constant.49.clone.1) | dynamic-update-slice | bytes 4194308 | tf_op jit(solution)/shard_map/dynamic_update_slice | solution.py:24
  50.4 5.6 %dynamic_update_slice.44 = f32[2,132,2048]{2,1,0:T(8,128)S(1)} dynamic-update-slice(f32[2,132,2048]{2,1,0:T(8,128)S(1)} %broadcast.39.clone, f32[2,128,2048]{2,1,0:T(8,128)} %broadcast_multiply_fusion.3, s32[]{:T(128)} %constant.49.clone.1, s32[]{:T(128)S(6)} %select_n.50, s32[]{:T(128)} %constant.49.clone.1) | dynamic-update-slice | bytes 4194308 | tf_op jit(solution)/shard_map/dynamic_update_slice | solution.py:24
  56.0 8.9 %multiply_add_fusion.2 = (f32[2,128,2048]{2,1,0:T(8,128)}, f32[2,128,2048]{2,1,0:T(8,128)}) fusion(f32[2,132,2048]{2,1,0:T(8,128)} %dynamic_update_slice.48, s32[]{:T(128)S(6)} %select_n.56, f32[]{:T(128)} %bitcast, f32[2,128,2047]{2,1,0:T(8,128)} %copy-done.3, f32[]{:T(128)} %bitcast.1, f32[1,128,2048]{2,1,0:T(8,128)} %copy-done.7, ...), kind=kLoop, calls=%fused_computation.29 | loop fusion | flops 6291456 | bytes 16775188 | tf_op jit(solution)/shard_map/dynamic_update_slice | solution.py:25
  64.9 5.5 %add.134 = f32[2,132,2048]{2,1,0:T(8,128)S(1)} dynamic-update-slice(f32[2,132,2048]{2,1,0:T(8,128)S(1)} %dynamic_update_slice.44, f32[2,128,2048]{2,1,0:T(8,128)} %get-tuple-element.43, s32[]{:T(128)} %constant.49.clone.1, s32[]{:T(128)S(6)} %select_n.51, s32[]{:T(128)} %constant.49.clone.1) | dynamic-update-slice | bytes 4194308 | tf_op jit(solution)/shard_map/add | solution.py:26
  70.4 7.5 %add.143 = f32[2,132,2048]{2,1,0:T(8,128)} dynamic-update-slice(f32[2,132,2048]{2,1,0:T(8,128)} %dynamic_update_slice.48, f32[2,128,2048]{2,1,0:T(8,128)} %get-tuple-element.42, s32[]{:T(128)} %constant.49.clone.1, s32[]{:T(128)S(6)} %select_n.56, s32[]{:T(128)} %constant.49.clone.1) | dynamic-update-slice | bytes 4194308 | tf_op jit(solution)/shard_map/add | solution.py:26
  78.6 3.7 %fusion = (f32[2,128,2047]{2,1,0:T(8,128)S(1)}, f32[2,128,2047]{2,1,0:T(8,128)}) fusion(f32[1,128,2048]{2,1,0:T(8,128)} %get-tuple-element.29, f32[1,128,2048]{2,1,0:T(8,128)} %get-tuple-element.22, f32[1,128,2048]{2,1,0:T(8,128)S(1)} %get-tuple-element.25, f32[1,128,2048]{2,1,0:T(8,128)} %get-tuple-element.26), kind=kLoop, calls=%fused_computation.15 | loop fusion | flops 1048064 | bytes 8386560 | tf_op jit(solution)/shard_map/stack | solution.py:19
  82.3 2.5 broadcast_multiply_fusion
  85.1 5.6 %dynamic_update_slice.56 = f32[2,132,2048]{2,1,0:T(8,128)S(1)} dynamic-update-slice(f32[2,132,2048]{2,1,0:T(8,128)S(1)} %broadcast.39.clone.3, f32[2,128,2048]{2,1,0:T(8,128)} %broadcast_multiply_fusion, s32[]{:T(128)} %constant.49.clone.1, s32[]{:T(128)S(6)} %select_n.62, s32[]{:T(128)} %constant.49.clone.1) | dynamic-update-slice | bytes 4194308 | tf_op jit(solution)/shard_map/dynamic_update_slice | solution.py:24
  90.6 5.5 %multiply_add_fusion = f32[2,128,2048]{2,1,0:T(8,128)} fusion(f32[2,132,2048]{2,1,0:T(8,128)S(1)} %dynamic_update_slice.56, s32[]{:T(128)S(6)} %select_n.63, f32[]{:T(128)} %bitcast.8, f32[2,128,2047]{2,1,0:T(8,128)} %copy-done.1, f32[]{:T(128)} %bitcast.9, f32[1,128,2048]{2,1,0:T(8,128)} %get-tuple-element.22, f32[1,128,2048]{2,1,0:T(8,128)} %get-tuple-element.29, ...), kind=kLoop, calls=%fused_computation.27 | loop fusion | flops 3145728 | bytes 8387600 | tf_op jit(solution)/shard_map/dynamic_update_slice | solution.py:25
  96.1 5.5 %add.159 = f32[2,132,2048]{2,1,0:T(8,128)S(1)} dynamic-update-slice(f32[2,132,2048]{2,1,0:T(8,128)S(1)} %dynamic_update_slice.56, f32[2,128,2048]{2,1,0:T(8,128)} %multiply_add_fusion, s32[]{:T(128)} %constant.49.clone.1, s32[]{:T(128)S(6)} %select_n.63, s32[]{:T(128)} %constant.49.clone.1) | dynamic-update-slice | bytes 4194308 | tf_op jit(solution)/shard_map/add | solution.py:26
  101.6 4.4 %broadcast_multiply_fusion.1 = f32[2,128,2048]{2,1,0:T(8,128)} fusion(f32[]{:T(128)S(6)} %sub.28, f32[2,128,2047]{2,1,0:T(8,128)} %get-tuple-element.45, f32[]{:T(128)} %bitcast.9, f32[1,128,2048]{2,1,0:T(8,128)S(1)} %get-tuple-element.25, f32[1,128,2048]{2,1,0:T(8,128)} %get-tuple-element.26, f32[]{:T(128)S(6)} %sub.29), kind=kLoop, calls=%fused_computation.37 | loop fusion | flops 2621440 | bytes 6290444 | tf_op jit(solution)/shard_map/mul | solution.py:24
  106.6 1.6 broadcast.39.clone.2
  108.3 7.2 %dynamic_update_slice.52 = f32[2,132,2048]{2,1,0:T(8,128)} dynamic-update-slice(f32[2,132,2048]{2,1,0:T(8,128)} %broadcast.39.clone.2, f32[2,128,2048]{2,1,0:T(8,128)} %broadcast_multiply_fusion.1, s32[]{:T(128)} %constant.49.clone.1, s32[]{:T(128)S(6)} %select_n.59, s32[]{:T(128)} %constant.49.clone.1) | dynamic-update-slice | bytes 4194308 | tf_op jit(solution)/shard_map/dynamic_update_slice | solution.py:24
  115.4 5.8 %multiply_add_fusion.1 = f32[2,128,2048]{2,1,0:T(8,128)} fusion(f32[2,132,2048]{2,1,0:T(8,128)} %dynamic_update_slice.52, s32[]{:T(128)S(6)} %select_n.60, f32[]{:T(128)} %bitcast.8, f32[2,128,2047]{2,1,0:T(8,128)} %get-tuple-element.45, f32[]{:T(128)} %bitcast.9, f32[1,128,2048]{2,1,0:T(8,128)S(1)} %get-tuple-element.25, ...), kind=kLoop, calls=%fused_computation.28 | loop fusion | flops 3145728 | bytes 8387600 | tf_op jit(solution)/shard_map/dynamic_update_slice | solution.py:25
  121.3 7.2 %add.151 = f32[2,132,2048]{2,1,0:T(8,128)} dynamic-update-slice(f32[2,132,2048]{2,1,0:T(8,128)} %dynamic_update_slice.52, f32[2,128,2048]{2,1,0:T(8,128)} %multiply_add_fusion.1, s32[]{:T(128)} %constant.49.clone.1, s32[]{:T(128)S(6)} %select_n.60, s32[]{:T(128)} %constant.49.clone.1) | dynamic-update-slice | bytes 4194308 | tf_op jit(solution)/shard_map/add | solution.py:26
  128.5 8.0 %broadcast_in_dim.3 = f32[2,516,4096]{2,1,0:T(8,128)} broadcast(f32[]{:T(128)} %constant.47.clone.1), dimensions={} | broadcast | bytes 16908292 | tf_op jit(solution)/shard_map/broadcast_in_dim | solution.py:31
  136.5 13.6 %dynamic_update_slice.47 = f32[2,516,4096]{2,1,0:T(8,128)} dynamic-update-slice(f32[2,516,4096]{2,1,0:T(8,128)} %broadcast_in_dim.3, f32[2,132,2048]{2,1,0:T(8,128)} %copy-done, s32[]{:T(128)} %constant.49.clone.1, s32[]{:T(128)S(6)} %select_n.52, s32[]{:T(128)S(6)} %select_n.53) | dynamic-update-slice | bytes 4325380 | tf_op jit(solution)/shard_map/dynamic_update_slice | solution.py:47
  150.0 4.3 %dynamic-slice_add_fusion.2 = f32[2,132,2048]{2,1,0:T(8,128)} fusion(f32[2,132,2048]{2,1,0:T(8,128)} %add.143, f32[2,516,4096]{2,1,0:T(8,128)} %dynamic_update_slice.47, s32[]{:T(128)S(6)} %select_n.54, s32[]{:T(128)S(6)} %select_n.53), kind=kLoop, calls=%fused_computation.14 | loop fusion | flops 540672 | bytes 6488072 | tf_op jit(solution)/shard_map/add | solution.py:47
  154.4 13.3 %dynamic_update_slice.51 = f32[2,516,4096]{2,1,0:T(8,128)} dynamic-update-slice(f32[2,516,4096]{2,1,0:T(8,128)} %dynamic_update_slice.47, f32[2,132,2048]{2,1,0:T(8,128)} %dynamic-slice_add_fusion.2, s32[]{:T(128)} %constant.49.clone.1, s32[]{:T(128)S(6)} %select_n.54, s32[]{:T(128)S(6)} %select_n.53) | dynamic-update-slice | bytes 4325380 | tf_op jit(solution)/shard_map/dynamic_update_slice | solution.py:47
  167.7 4.4 %dynamic-slice_add_fusion.1 = f32[2,132,2048]{2,1,0:T(8,128)} fusion(f32[2,132,2048]{2,1,0:T(8,128)} %add.151, f32[2,516,4096]{2,1,0:T(8,128)} %dynamic_update_slice.51, s32[]{:T(128)S(6)} %select_n.57, s32[]{:T(128)S(6)} %select_n.58), kind=kLoop, calls=%fused_computation.13 | loop fusion | flops 540672 | bytes 6488072 | tf_op jit(solution)/shard_map/add | solution.py:47
  172.0 13.4 %dynamic_update_slice.55 = f32[2,516,4096]{2,1,0:T(8,128)} dynamic-update-slice(f32[2,516,4096]{2,1,0:T(8,128)} %dynamic_update_slice.51, f32[2,132,2048]{2,1,0:T(8,128)} %dynamic-slice_add_fusion.1, s32[]{:T(128)} %constant.49.clone.1, s32[]{:T(128)S(6)} %select_n.57, s32[]{:T(128)S(6)} %select_n.58) | dynamic-update-slice | bytes 4325380 | tf_op jit(solution)/shard_map/dynamic_update_slice | solution.py:47
  185.5 3.7 %dynamic-slice_add_fusion = f32[2,132,2048]{2,1,0:T(8,128)} fusion(f32[2,132,2048]{2,1,0:T(8,128)S(1)} %add.159, f32[2,516,4096]{2,1,0:T(8,128)} %dynamic_update_slice.55, s32[]{:T(128)S(6)} %select_n.61, s32[]{:T(128)S(6)} %select_n.58), kind=kLoop, calls=%fused_computation.12 | loop fusion | flops 540672 | bytes 6488072 | tf_op jit(solution)/shard_map/add | solution.py:47
  189.2 13.4 %dynamic_update_slice.59 = f32[2,516,4096]{2,1,0:T(8,128)} dynamic-update-slice(f32[2,516,4096]{2,1,0:T(8,128)} %dynamic_update_slice.55, f32[2,132,2048]{2,1,0:T(8,128)} %dynamic-slice_add_fusion, s32[]{:T(128)} %constant.49.clone.1, s32[]{:T(128)S(6)} %select_n.61, s32[]{:T(128)S(6)} %select_n.58) | dynamic-update-slice | bytes 4325380 | tf_op jit(solution)/shard_map/dynamic_update_slice | solution.py:47
  203.6 4.7 %collective-permute-start = (f32[2,4,4096]{2,1,0:T(4,128)S(1)}, f32[2,4,4096]{2,1,0:T(4,128)S(1)}, u32[]{:S(2)}, u32[]{:S(2)}) collective-permute-start(f32[2,4,4096]{2,1,0:T(4,128)S(1)} %slice.156), channel_id=1, source_target_pairs={{0,1},{1,2},{2,3},{4,5},{5,6},{6,7},{8,9},{9,10},{10,11},{12,13},{... | collective-permute-start | bytes 393224 | tf_op jit(solution)/shard_map/ppermute | solution.py:15
  208.3 11.6 %slice.154 = f32[2,512,4096]{2,1,0:T(8,128)} slice(f32[2,516,4096]{2,1,0:T(8,128)} %dynamic_update_slice.59), slice={[0:2], [0:512], [0:4096]} | slice | bytes 33554432 | tf_op jit(solution)/shard_map/slice | solution.py:49
  219.8 1.7 fusion.12
  221.5 116.2 %reduce-scatter.2.cloned.1.call-done = f32[2,512,512]{2,1,0:T(8,128)} async-done(((f32[2,512,4096]{2,1,0:T(8,128)}), f32[2,512,512]{2,1,0:T(8,128)}) %reduce-scatter.2.cloned.1.call-update) | async-done | bytes 2097168 | tf_op jit(solution)/shard_map/reduce_scatter | solution.py:50
  337.7 3.4 maximum_divide_fusion
  (33 shorter events, 10.1 us)
Async XLA Ops:
  7.2 330.5 %reduce-scatter.2.cloned.1.call-start = ((), (), s32[]{:S(2)}) async-start(), calls=%async_computation.1 | async-start | bytes 18874368 | tf_op jit(solution)/shard_map/reduce_scatter | solution.py:50
  34.6 1.0 copy-start.7
  34.6 1.4 copy-start.9
  34.6 2.7 copy-start.6
  34.6 2.7 copy-start.8
  34.8 2.6 copy-start.2
  36.0 1.9 copy-start.3
  70.4 7.5 %copy-start = (f32[2,132,2048]{2,1,0:T(8,128)}, f32[2,132,2048]{2,1,0:T(8,128)S(1)}, u32[]{:S(2)}) copy-start(f32[2,132,2048]{2,1,0:T(8,128)S(1)} %add.134) | copy-start | bytes 6488068
  78.6 3.7 %copy-start.4 = (f32[1,128,2048]{2,1,0:T(8,128)S(1)}, f32[1,128,2048]{2,1,0:T(8,128)}, u32[]{:S(2)}) copy-start(f32[1,128,2048]{2,1,0:T(8,128)} %get-tuple-element.22) | copy-start | bytes 3145732
  78.6 3.7 %copy-start.5 = (f32[1,128,2048]{2,1,0:T(8,128)S(1)}, f32[1,128,2048]{2,1,0:T(8,128)}, u32[]{:S(2)}) copy-start(f32[1,128,2048]{2,1,0:T(8,128)} %get-tuple-element.29) | copy-start | bytes 3145732
  82.3 2.6 copy-start.1
  203.6 16.3 %collective-permute-start = (f32[2,4,4096]{2,1,0:T(4,128)S(1)}, f32[2,4,4096]{2,1,0:T(4,128)S(1)}, u32[]{:S(2)}, u32[]{:S(2)}) collective-permute-start(f32[2,4,4096]{2,1,0:T(4,128)S(1)} %slice.156), channel_id=1, source_target_pairs={{0,1},{1,2},{2,3},{4,5},{5,6},{6,7},{8,9},{9,10},{10,11},{12,13},{... | collective-permute-start | bytes 393224 | tf_op jit(solution)/shard_map/ppermute | solution.py:15
Sparse Core Ops, SparseCore 0:
  221.7 115.9 reduce-scatter.1
where the time goes:
time: 352 us; the launch traced here: 348 us
  local copies, waits for them, and re-layouts  137 us (39%)
  waiting for transfers between devices  116 us (33%)
  other arithmetic  58.3 us (17%)
  between operations  31.4 us (9%)
  starting transfers between devices  4.73 us (1%)
    reduce_scatter x1, waiting for transfers between devices, body(): summed = lax.psum_scatter(owned, 'pgroup', scatter_dimension=2, tiled=True)  116 us
    dynamic_update_slice x4, local copies, waits for them, and re-layouts, body(): lax.dynamic_update_slice(canvas, old + piece, (zero, row_start, col_start))  53.7 us
    add x4, local copies, waits for them, and re-layouts, contribution(): return first + second  25.8 us
    dynamic_update_slice x4, local copies, waits for them, and re-layouts, contribution(): lax.dynamic_update_slice(empty, (1.0 - row_f) * banded, (zero, shift, zero))  25 us
    dynamic_update_slice x3, other arithmetic, contribution(): lax.dynamic_update_slice(empty, row_f * banded, (zero, shift + 1, zero))  20.2 us
    add x3, other arithmetic, body(): old + piece  12.4 us
    slice x1, local copies, waits for them, and re-layouts, body(): owned = canvas[:, :own_rows].at[:, :HALO].add(border)  11.6 us
    mul x4, other arithmetic, contribution(): (1.0 - row_f) * banded  10.9 us
  transfers between devices with their start and end apart: 2, of which 1 were waited for; matrix products, arithmetic and copies ran while one was open for 3% of the time, Pallas kernels for 0%

commit v1 on v0

v1 whole, which is shorter than its diff:
```python
import functools
import math

import jax
import jax.numpy as jnp
from jax import lax
from jax.experimental import pallas as pl
from jax.experimental.pallas import tpu as pltpu
from jax.sharding import PartitionSpec as P

TILE_BLOCKS = 4
SKY_COLS = 4096
HALO = 4
LANES = 128
BLOCK = 128
ROWS = 64
TALL = BLOCK + 8
MESH = pl.DeviceIdType.MESH
F32 = jnp.float32


def chip_grid(groups):
    chips = groups // 2
    along_x = math.isqrt(chips)
    while chips % along_x:
        along_x -= 1
    return chips // along_x, along_x


def kernel(
    ny, nx, n_tile,
    images, beams, row_block, col_block, band, row_frac, col_frac,
    out,
    raw_i, raw_b, mid, placed, halo_out, halo_in, give, take, canvas,
    first_a, first_b, second_a, second_b, last,
    load_sem, halo_sem, swap_sem, first_sem, second_sem, last_sem,
):
    points, img_rows, width = images.shape
    blocks = img_rows // BLOCK
    col_tiles = width // LANES
    sky_tiles = SKY_COLS // LANES
    own = sky_tiles // (ny * nx)
    half = own // 2
    pairs = TILE_BLOCKS
    per_array = points * blocks * col_tiles
    empty = 2 * per_array

    me = lax.axis_index("pgroup")
    tile = lax.axis_index("tile")
    core = lax.rem(me, 2)
    chip = me // 2
    x = lax.rem(chip, nx)
    y = chip // nx
    partner = me + 1 - 2 * core
    x_peers = [(y * nx + lax.rem(x + d, nx)) * 2 + core for d in range(1, nx)]
    y_peers = [(lax.rem(y + d, ny) * nx + x) * 2 + core for d in range(1, ny)]
    after = lax.rem(tile + 1, n_tile)
    before = lax.rem(tile + n_tile - 1, n_tile)

    loads = []
    for p in range(points):
        for b in range(blocks):
            for which, (source, target) in enumerate(((images, raw_i), (beams, raw_b))):
                rows = pl.ds(b * BLOCK, BLOCK)
                copy = pltpu.make_async_copy(
                    source.at[p, rows], target.at[p, rows], load_sem.at[which, p * blocks + b]
                )
                copy.start()
                loads.append(copy)

    barrier = pltpu.get_barrier_semaphore()
    near = [{"pgroup": q} for q in [partner] + x_peers + y_peers]
    near += [{"tile": after}, {"tile": before}]
    for device in near:
        pl.semaphore_signal(barrier, inc=1, device_id=device, device_id_type=MESH)

    placed[empty] = jnp.zeros((TALL, LANES), F32)
    for slot in range(4):
        mid[slot, :8] = jnp.zeros((8, LANES), F32)
        mid[slot, 8 + BLOCK :] = jnp.zeros((8, LANES), F32)
    first_lane = lax.broadcasted_iota(jnp.int32, (BLOCK, LANES), 1) == 0

    for p in range(points):
        f = row_frac[p]
        g = col_frac[p]
        for b in range(blocks):
            loads[2 * (p * blocks + b)].wait()
            loads[2 * (p * blocks + b) + 1].wait()
            shift = band[p, b]
            rows = pl.ds(b * BLOCK, BLOCK)

            def tile_pair(step, _, p=p, b=b, f=f, g=g, shift=shift, rows=rows):
                for sub in range(2):
                    t = 2 * step + sub
                    lanes = pl.ds(pl.multiple_of(t * LANES, LANES), LANES)
                    left = pl.ds(pl.multiple_of(jnp.maximum(t - 1, 0) * LANES, LANES), LANES)
                    there = jnp.where(t > 0, g, 0.0)
                    beam = raw_b[p, rows, lanes]
                    beam_left = raw_b[p, rows, left]
                    for a, other in enumerate((raw_i, raw_b)):
                        here = beam * other[p, rows, lanes]
                        prior = beam_left * other[p, rows, left]
                        moved = jnp.where(
                            first_lane,
                            there * pltpu.roll(prior, 1, 1),
                            g * pltpu.roll(here, 1, 1),
                        )
                        slot = 2 * sub + a
                        mid[slot, 8 : 8 + BLOCK] = (1.0 - g) * here + moved
                        low = mid[slot, pl.ds(8 - shift, TALL)]
                        high = mid[slot, pl.ds(7 - shift, TALL)]
                        index = a * per_array + (p * blocks + b) * col_tiles + t
                        placed[index] = (1.0 - f) * low + f * high
                return 0

            lax.fori_loop(0, col_tiles // 2, tile_pair, 0)

    def where_placed(a, p, sky_block, sky_tile):
        b = sky_block - (row_block[p] - tile * TILE_BLOCKS)
        t = sky_tile - col_block[p]
        inside = (b >= 0) & (b < blocks) & (t >= 0) & (t < col_tiles)
        index = a * per_array + (p * blocks + b) * col_tiles + t
        return jnp.where(inside, index, empty)

    def slot_of(sky_tile, x_major):
        if not x_major:
            return sky_tile
        owner = sky_tile // own
        return (lax.rem(owner, nx) * ny + owner // nx) * own + lax.rem(sky_tile, own)

    def gather(a, sky_block, sky_tile, lower):
        start = ROWS if lower else 0
        total = None
        for p in range(points):
            term = placed[where_placed(a, p, sky_block, sky_tile), start : start + ROWS]
            total = term if total is None else total + term
        if lower:
            return total, None
        top = total[:8]
        for p in range(points):
            top = top + placed[where_placed(a, p, sky_block - 1, sky_tile), BLOCK:TALL]
        return total, top

    def border(sky_tile, _):
        for a in range(2):
            top = None
            for p in range(points):
                term = placed[where_placed(a, p, TILE_BLOCKS - 1, sky_tile), BLOCK:TALL]
                top = term if top is None else top + term
            halo_out[a, sky_tile] = top
        return 0

    lax.fori_loop(0, sky_tiles, border, 0)
    pl.semaphore_wait(barrier, len(near))

    halo = pltpu.make_async_remote_copy(
        halo_out, halo_in, halo_sem.at[0], halo_sem.at[1],
        device_id={"tile": after}, device_id_type=MESH,
    )
    halo.start()

    def swap(k):
        return pltpu.make_async_remote_copy(
            give.at[k], take.at[k], swap_sem.at[0, k], swap_sem.at[1, k],
            device_id={"pgroup": partner}, device_id_type=MESH,
        )

    def build(k, j, lower):
        sky_block = pairs - 1 - j
        other = 1 - core

        def one(sky_tile, _):
            total, top = gather(other, sky_block, sky_tile, lower)
            slot = slot_of(sky_tile, lower)
            give[k, slot] = total
            if top is not None:
                give[k, slot, :8] = top
            return 0

        lax.fori_loop(0, sky_tiles, one, 0, unroll=2)
        if not lower:
            @pl.when(j == pairs - 1)
            def _():
                halo.wait_recv()
                use = jnp.where(tile > 0, 1.0, 0.0)

                def add(s, _):
                    give[k, s, :8] += use * halo_in[other, s]
                    return 0

                lax.fori_loop(0, sky_tiles, add, 0, unroll=4)
        swap(k).start()

    def first_copies(k, j, lower):
        copies = []
        count, at, peers = (nx, x, x_peers) if lower else (ny, y, y_peers)
        size = sky_tiles // count
        target = first_a if lower else first_b
        for d in range(1, count):
            to = lax.rem(at + d, count)
            copies.append(pltpu.make_async_remote_copy(
                canvas.at[k, pl.ds(to * size, size)], target.at[j, d - 1],
                first_sem.at[0, k, d - 1], first_sem.at[1, k, d - 1],
                device_id={"pgroup": peers[d - 1]}, device_id_type=MESH,
            ))
        return copies

    def second_copies(k, j, lower):
        copies = []
        count, at, peers = (ny, y, y_peers) if lower else (nx, x, x_peers)
        base = (x * ny if lower else y * nx) * own
        target = second_a if lower else second_b
        for d in range(1, count):
            to = lax.rem(at + d, count)
            copies.append(pltpu.make_async_remote_copy(
                canvas.at[k, pl.ds(base + to * own, own)], target.at[j, d - 1],
                second_sem.at[0, k, d - 1], second_sem.at[1, k, d - 1],
                device_id={"pgroup": peers[d - 1]}, device_id_type=MESH,
            ))
        return copies

    def combine(k, j, lower):
        sky_block = pairs - 1 - j
        swap(k).wait_recv()

        def one(sky_tile, _):
            total, top = gather(core, sky_block, sky_tile, lower)
            slot = slot_of(sky_tile, lower)
            canvas[k, slot] = total + take[k, slot]
            if top is not None:
                canvas[k, slot, :8] = top + take[k, slot, :8]
            return 0

        lax.fori_loop(0, sky_tiles, one, 0, unroll=2)
        if not lower:
            @pl.when(j == pairs - 1)
            def _():
                use = jnp.where(tile > 0, 1.0, 0.0)

                def add(s, _):
                    canvas[k, s, :8] += use * halo_in[core, s]
                    return 0

                lax.fori_loop(0, sky_tiles, add, 0, unroll=4)
        for copy in first_copies(k, j, lower):
            copy.start()

    build(0, 0, True)
    build(1, 0, False)

    def spread(j, _):
        for lower in (True, False):
            k = 2 * j + (0 if lower else 1)
            combine(k, j, lower)

            @pl.when(j < pairs - 1)
            def _():
                build(k + 2, j + 1, lower)
        return 0

    lax.fori_loop(0, pairs, spread, 0)

    def middle(j, _):
        for lower in (True, False):
            k = 2 * j + (0 if lower else 1)
            copies = first_copies(k, j, lower)
            for copy in copies:
                copy.wait_recv()
            count, at = (nx, x) if lower else (ny, y)
            size = sky_tiles // count
            source = first_a if lower else first_b

            def one(s, _):
                total = canvas[k, at * size + s]
                for d in range(count - 1):
                    total = total + source[j, d, s]
                canvas[k, at * size + s] = total
                return 0

            lax.fori_loop(0, size, one, 0, unroll=2)
            for copy in second_copies(k, j, lower):
                copy.start()
        return 0

    lax.fori_loop(0, pairs, middle, 0)

    def mine(lower):
        return (x * ny + y if lower else y * nx + x) * own

    def last_copy(k, lower):
        return pltpu.make_async_remote_copy(
            canvas.at[k, pl.ds(mine(lower) + (1 - core) * half, half)], last.at[k],
            last_sem.at[0, k], last_sem.at[1, k],
            device_id={"pgroup": partner}, device_id_type=MESH,
        )

    def finish(j, _):
        for lower in (True, False):
            k = 2 * j + (0 if lower else 1)
            for copy in second_copies(k, j, lower):
                copy.wait_recv()
            source = second_a if lower else second_b
            count = ny if lower else nx
            row = (pairs - 1 - j) * BLOCK + (ROWS if lower else 0)
            rows = pl.ds(pl.multiple_of(row, ROWS), ROWS)

            def summed(s):
                total = canvas[k, mine(lower) + s]
                for d in range(count - 1):
                    total = total + source[j, d, s]
                return total

            for s in range(half):
                canvas[k, mine(lower) + (1 - core) * half + s] = summed((1 - core) * half + s)
            last_copy(k, lower).start()
            for s in range(half):
                out[core, rows, s * LANES : (s + 1) * LANES] = summed(core * half + s)
        return 0

    lax.fori_loop(0, pairs, finish, 0)

    def receive(j, _):
        for lower in (True, False):
            k = 2 * j + (0 if lower else 1)
            last_copy(k, lower).wait()
            row = (pairs - 1 - j) * BLOCK + (ROWS if lower else 0)
            rows = pl.ds(pl.multiple_of(row, ROWS), ROWS)
            for s in range(half):
                out[1 - core, rows, s * LANES : (s + 1) * LANES] = last[k, s]
            swap(k).wait_send()
            for copy in first_copies(k, j, lower) + second_copies(k, j, lower):
                copy.wait_send()
        return 0

    lax.fori_loop(0, pairs, receive, 0)
    halo.wait_send()


def body(ny, nx, n_tile, images, beams, row_block, col_block, band, row_frac, col_frac):
    points, img_rows, width = images.shape
    blocks = img_rows // BLOCK
    col_tiles = width // LANES
    sky_tiles = SKY_COLS // LANES
    own = sky_tiles // (ny * nx)
    pairs = TILE_BLOCKS
    chunks = 2 * pairs
    own_cols = SKY_COLS // (2 * ny * nx)
    most = max(nx, ny) - 1
    dma = pltpu.SemaphoreType.DMA
    smem = pl.BlockSpec(memory_space=pltpu.SMEM)
    summed = pl.pallas_call(
        functools.partial(kernel, ny, nx, n_tile),
        out_shape=jax.ShapeDtypeStruct((2, TILE_BLOCKS * BLOCK, own_cols), F32),
        in_specs=[pl.BlockSpec(memory_space=pl.ANY)] * 2 + [smem] * 5,
        out_specs=pl.BlockSpec(memory_space=pltpu.VMEM),
        scratch_shapes=[
            pltpu.VMEM((points, img_rows, width), F32),
            pltpu.VMEM((points, img_rows, width), F32),
            pltpu.VMEM((4, BLOCK + 16, LANES), F32),
            pltpu.VMEM((2 * points * blocks * col_tiles + 1, TALL, LANES), F32),
            pltpu.VMEM((2, sky_tiles, 8, LANES), F32),
            pltpu.VMEM((2, sky_tiles, 8, LANES), F32),
            pltpu.VMEM((chunks, sky_tiles, ROWS, LANES), F32),
            pltpu.VMEM((chunks, sky_tiles, ROWS, LANES), F32),
            pltpu.VMEM((chunks, sky_tiles, ROWS, LANES), F32),
            pltpu.VMEM((pairs, nx - 1, sky_tiles // nx, ROWS, LANES), F32),
            pltpu.VMEM((pairs, ny - 1, sky_tiles // ny, ROWS, LANES), F32),
            pltpu.VMEM((pairs, ny - 1, own, ROWS, LANES), F32),
            pltpu.VMEM((pairs, nx - 1, own, ROWS, LANES), F32),
            pltpu.VMEM((chunks, own // 2, ROWS, LANES), F32),
            dma((2, points * blocks)),
            dma((2,)),
            dma((2, chunks)),
            dma((2, chunks, most)),
            dma((2, chunks, most)),
            dma((2, chunks)),
        ],
        compiler_params=pltpu.CompilerParams(
            collective_id=0, has_side_effects=True, vmem_limit_bytes=67043328
        ),
        name="combine",
    )(images, beams, row_block, col_block, band, row_frac, col_frac)
    numer = summed[0]
    weight = summed[1]
    normalised = numer / jnp.maximum(weight, 0.05)
    return (numer, weight, normalised)


def solution(mesh):
    ny, nx = chip_grid(mesh.shape["pgroup"])
    return jax.shard_map(
        functools.partial(body, ny, nx, mesh.shape["tile"]),
        mesh=mesh,
        in_specs=(
            P(("pgroup", "tile"), None, None),
            P(("pgroup", "tile"), None, None),
            P(("pgroup", "tile")),
            P(("pgroup", "tile")),
            P(("pgroup", "tile"), None),
            P(("pgroup", "tile")),
            P(("pgroup", "tile")),
        ),
        out_specs=(P("tile", "pgroup"), P("tile", "pgroup"), P("tile", "pgroup")),
        check_vma=False,
    )
```

time: 352 us -> 94.2 us (0.27); the launches traced: 348 us -> 94.1 us
  local copies, waits for them, and re-layouts: 137 us -> 0 us
  waiting for transfers between devices: 116 us -> 0 us
  Pallas kernels: 0 us -> 90 us
  other arithmetic: 58.3 us -> 3.39 us
  between operations: 31.4 us -> 0.64 us
  starting transfers between devices: 4.73 us -> 0 us
    reduce_scatter x1 -> x0, waiting for transfers between devices: 116 us -> none  [body(): summed = lax.psum_scatter(owned, 'pgroup', scatter_dimension=2, tiled=True)]
    pallas_call x0 -> x1, Pallas kernels: none -> 90 us  [body(): pl.pallas_call(functools.partial(kernel, ny, nx, n_tile), out_shape=jax.S...]
    dynamic_update_slice x8 -> x0, local copies, waits for them, and re-layouts: 78.7 us -> none  [the longest x4 53.7 us: body(): lax.dynamic_update_slice(canvas, old + piece, (zero, row_start, col_start))]
    add x4 -> x0, local copies, waits for them, and re-layouts: 25.8 us -> none  [contribution(): return first + second]
    dynamic_update_slice x3 -> x0, other arithmetic: 20.2 us -> none  [contribution(): lax.dynamic_update_slice(empty, row_f * banded, (zero, shift + 1, zero))]
    slice x7 -> x0, local copies, waits for them, and re-layouts: 19.4 us -> none  [the longest x1 11.6 us: body(): owned = canvas[:, :own_rows].at[:, :HALO].add(border)]
    mul x5 -> x0, other arithmetic: 16.7 us -> none  [the longest x4 10.9 us: contribution(): (1.0 - row_f) * banded]
    add x3 -> x0, other arithmetic: 12.4 us -> none  [body(): old + piece]
  transfers between devices with their start and end apart: 2 -> 0, of which waited for: 1 -> 0; matrix products, arithmetic and copies ran while one was open for 3% -> 0% of each run, Pallas kernels for 0% -> 0%
where the time goes in v1:
time: 94.2 us; the launch traced here: 94.1 us
  Pallas kernels  90 us (96%)
  other arithmetic  3.39 us (4%)
    pallas_call x1, Pallas kernels, body(): pl.pallas_call(functools.partial(kernel, ny, nx, n_tile), out_shape=jax.S...  90 us
    div x1, other arithmetic, body(): normalised = numer / jnp.maximum(weight, 0.05)  3.39 us

profile of v1, /device:TPU:0, one launch (start us, length us, event | category | flops | bytes accessed | tf_op | source)
XLA Modules:
  0.0 94.1 jit_solution(17637305359761588451)
XLA Ops:
  0.6 90.0 %combine.1 = f32[2,512,512]{2,1,0:T(8,128)} custom-call(f32[2,256,2048]{2,1,0:T(8,128)} %images.1, f32[2,256,2048]{2,1,0:T(8,128)} %beams.1, s32[2]{0:T(128)} %row_block.1, s32[2]{0:T(128)} %col_block.1, s32[2,2]{1,0:T(2,128)} %band.1, f32[2]{0:T(128)} %row_frac.1, f32[2]{0:T(128)} %col_frac.1), custom_call_target="tpu_custom_call" | custom-call | tf_op jit(solution)/shard_map/combine/pallas_call | solution.py:351
  90.7 3.4 %maximum_divide_fusion = (f32[512,512]{1,0:T(8,128)}, f32[512,512]{1,0:T(8,128)}, f32[512,512]{1,0:T(8,128)}) fusion(f32[2,512,512]{2,1,0:T(8,128)} %combine.1), kind=kLoop, calls=%fused_computation | loop fusion | flops 524288 | bytes 5242880 | tf_op jit(solution)/shard_map/div | solution.py:385

commit v2 on v1

--- a/solution.py
+++ b/solution.py
@@ -13,8 +13,11 @@
 HALO = 4
 LANES = 128
 BLOCK = 128
-ROWS = 64
+ROWS = 32
+PER_BLOCK = BLOCK // (2 * ROWS)
 TALL = BLOCK + 8
+AHEAD = 2
+LAG = 2
 MESH = pl.DeviceIdType.MESH
 F32 = jnp.float32
 
@@ -31,9 +34,10 @@
     ny, nx, n_tile,
     images, beams, row_block, col_block, band, row_frac, col_frac,
     out,
-    raw_i, raw_b, mid, placed, halo_out, halo_in, give, take, canvas,
+    raw, mid, placed, halo_out, halo_in, give, take, canvas,
     first_a, first_b, second_a, second_b, last,
-    load_sem, halo_sem, swap_sem, first_sem, second_sem, last_sem,
+    ready,
+    load_sem, halo_sem, swap_sem, first_sem, second_sem, last_sem, out_sem,
 ):
     points, img_rows, width = images.shape
     blocks = img_rows // BLOCK
@@ -41,7 +45,7 @@
     sky_tiles = SKY_COLS // LANES
     own = sky_tiles // (ny * nx)
     half = own // 2
-    pairs = TILE_BLOCKS
+    pairs = TILE_BLOCKS * PER_BLOCK
     per_array = points * blocks * col_tiles
     empty = 2 * per_array
 
@@ -57,16 +61,16 @@
     after = lax.rem(tile + 1, n_tile)
     before = lax.rem(tile + n_tile - 1, n_tile)
 
-    loads = []
-    for p in range(points):
-        for b in range(blocks):
-            for which, (source, target) in enumerate(((images, raw_i), (beams, raw_b))):
+    loads = {}
+    for b in reversed(range(blocks)):
+        for p in range(points):
+            for which, source in enumerate((images, beams)):
                 rows = pl.ds(b * BLOCK, BLOCK)
                 copy = pltpu.make_async_copy(
-                    source.at[p, rows], target.at[p, rows], load_sem.at[which, p * blocks + b]
+                    source.at[p, rows], raw.at[which, p, rows], load_sem.at[which, p * blocks + b]
                 )
                 copy.start()
-                loads.append(copy)
+                loads[which, p, b] = copy
 
     barrier = pltpu.get_barrier_semaphore()
     near = [{"pgroup": q} for q in [partner] + x_peers + y_peers]
@@ -78,42 +82,40 @@
     for slot in range(4):
         mid[slot, :8] = jnp.zeros((8, LANES), F32)
         mid[slot, 8 + BLOCK :] = jnp.zeros((8, LANES), F32)
-    first_lane = lax.broadcasted_iota(jnp.int32, (BLOCK, LANES), 1) == 0
-
-    for p in range(points):
-        f = row_frac[p]
-        g = col_frac[p]
-        for b in range(blocks):
-            loads[2 * (p * blocks + b)].wait()
-            loads[2 * (p * blocks + b) + 1].wait()
-            shift = band[p, b]
-            rows = pl.ds(b * BLOCK, BLOCK)
-
-            def tile_pair(step, _, p=p, b=b, f=f, g=g, shift=shift, rows=rows):
-                for sub in range(2):
-                    t = 2 * step + sub
-                    lanes = pl.ds(pl.multiple_of(t * LANES, LANES), LANES)
-                    left = pl.ds(pl.multiple_of(jnp.maximum(t - 1, 0) * LANES, LANES), LANES)
-                    there = jnp.where(t > 0, g, 0.0)
-                    beam = raw_b[p, rows, lanes]
-                    beam_left = raw_b[p, rows, left]
-                    for a, other in enumerate((raw_i, raw_b)):
-                        here = beam * other[p, rows, lanes]
-                        prior = beam_left * other[p, rows, left]
-                        moved = jnp.where(
-                            first_lane,
-                            there * pltpu.roll(prior, 1, 1),
-                            g * pltpu.roll(here, 1, 1),
-                        )
-                        slot = 2 * sub + a
-                        mid[slot, 8 : 8 + BLOCK] = (1.0 - g) * here + moved
-                        low = mid[slot, pl.ds(8 - shift, TALL)]
-                        high = mid[slot, pl.ds(7 - shift, TALL)]
+    last_lane = lax.broadcasted_iota(jnp.int32, (BLOCK, LANES), 1) == LANES - 1
+
+    def interpolate(a, fresh, some):
+        for b in some:
+            for p in range(points):
+                f = row_frac[p]
+                g = col_frac[p]
+                if fresh:
+                    loads[0, p, b].wait()
+                    loads[1, p, b].wait()
+                shift = band[p, b]
+                rows = pl.ds(b * BLOCK, BLOCK)
+
+                def some_tiles(step, _, p=p, b=b, f=f, g=g, shift=shift, rows=rows):
+                    for sub in range(4):
+                        t = 4 * step + sub
+                        lanes = pl.ds(pl.multiple_of(t * LANES, LANES), LANES)
+                        here = raw[1, p, rows, lanes] * raw[a, p, rows, lanes]
+                        if sub == 0:
+                            left = pl.ds(pl.multiple_of(jnp.maximum(t - 1, 0) * LANES, LANES), LANES)
+                            there = jnp.where(t > 0, 1.0, 0.0)
+                            prior = raw[1, p, rows, left] * raw[a, p, rows, left] * there
+                        else:
+                            left = pl.ds(pl.multiple_of((t - 1) * LANES, LANES), LANES)
+                            prior = raw[1, p, rows, left] * raw[a, p, rows, left]
+                        moved = pltpu.roll(jnp.where(last_lane, prior, here), 1, 1)
+                        mid[sub, 8 : 8 + BLOCK] = (1.0 - g) * here + g * moved
+                        low = mid[sub, pl.ds(8 - shift, TALL)]
+                        high = mid[sub, pl.ds(7 - shift, TALL)]
                         index = a * per_array + (p * blocks + b) * col_tiles + t
                         placed[index] = (1.0 - f) * low + f * high
-                return 0
-
-            lax.fori_loop(0, col_tiles // 2, tile_pair, 0)
+                    return 0
+
+                lax.fori_loop(0, col_tiles // 4, some_tiles, 0)
 
     def where_placed(a, p, sky_block, sky_tile):
         b = sky_block - (row_block[p] - tile * TILE_BLOCKS)
@@ -128,17 +130,25 @@
         owner = sky_tile // own
         return (lax.rem(owner, nx) * ny + owner // nx) * own + lax.rem(sky_tile, own)
 
-    def gather(a, sky_block, sky_tile, lower):
-        start = ROWS if lower else 0
+    def place_of(m, lower):
+        m = jnp.int32(m)
+        sky_block = TILE_BLOCKS - 1 - m // PER_BLOCK
+        turn = lax.rem(m, PER_BLOCK)
+        start = BLOCK - ROWS * (2 * turn + (1 if lower else 2))
+        return sky_block, pl.multiple_of(start, ROWS)
+
+    def gather(a, m, sky_tile, lower):
+        sky_block, start = place_of(m, lower)
         total = None
         for p in range(points):
-            term = placed[where_placed(a, p, sky_block, sky_tile), start : start + ROWS]
+            term = placed[where_placed(a, p, sky_block, sky_tile), pl.ds(start, ROWS)]
             total = term if total is None else total + term
         if lower:
             return total, None
         top = total[:8]
         for p in range(points):
-            top = top + placed[where_placed(a, p, sky_block - 1, sky_tile), BLOCK:TALL]
+            index = jnp.where(start == 0, where_placed(a, p, sky_block - 1, sky_tile), empty)
+            top = top + placed[index, BLOCK:TALL]
         return total, top
 
     def border(sky_tile, _):
@@ -150,14 +160,10 @@
             halo_out[a, sky_tile] = top
         return 0
 
-    lax.fori_loop(0, sky_tiles, border, 0)
-    pl.semaphore_wait(barrier, len(near))
-
     halo = pltpu.make_async_remote_copy(
         halo_out, halo_in, halo_sem.at[0], halo_sem.at[1],
         device_id={"tile": after}, device_id_type=MESH,
     )
-    halo.start()
 
     def swap(k):
         return pltpu.make_async_remote_copy(
@@ -166,11 +172,10 @@
         )
 
     def build(k, j, lower):
-        sky_block = pairs - 1 - j
         other = 1 - core
 
         def one(sky_tile, _):
-            total, top = gather(other, sky_block, sky_tile, lower)
+            total, top = gather(other, j, sky_tile, lower)
             slot = slot_of(sky_tile, lower)
             give[k, slot] = total
             if top is not None:
@@ -179,7 +184,7 @@
 
         lax.fori_loop(0, sky_tiles, one, 0, unroll=2)
         if not lower:
-            @pl.when(j == pairs - 1)
+            @pl.when(jnp.int32(j) == pairs - 1)
             def _():
                 halo.wait_recv()
                 use = jnp.where(tile > 0, 1.0, 0.0)
@@ -220,11 +225,10 @@
         return copies
 
     def combine(k, j, lower):
-        sky_block = pairs - 1 - j
         swap(k).wait_recv()
 
         def one(sky_tile, _):
-            total, top = gather(core, sky_block, sky_tile, lower)
+            total, top = gather(core, j, sky_tile, lower)
             slot = slot_of(sky_tile, lower)
             canvas[k, slot] = total + take[k, slot]
             if top is not None:
@@ -233,7 +237,7 @@
 
         lax.fori_loop(0, sky_tiles, one, 0, unroll=2)
         if not lower:
-            @pl.when(j == pairs - 1)
+            @pl.when(jnp.int32(j) == pairs - 1)
             def _():
                 use = jnp.where(tile > 0, 1.0, 0.0)
 
@@ -245,20 +249,36 @@
         for copy in first_copies(k, j, lower):
             copy.start()
 
+    groups = [[blocks - 1], list(reversed(range(blocks - 1)))]
+    interpolate(1 - core, True, groups[0])
+    pl.semaphore_wait(barrier, len(near))
     build(0, 0, True)
     build(1, 0, False)
+    interpolate(core, False, groups[0])
+    combine(0, 0, True)
+    combine(1, 0, False)
+    interpolate(1 - core, True, groups[1])
+    for m in range(1, 1 + AHEAD):
+        build(2 * m, m, True)
+        build(2 * m + 1, m, False)
+    interpolate(core, False, groups[1])
 
     def spread(j, _):
         for lower in (True, False):
-            k = 2 * j + (0 if lower else 1)
-            combine(k, j, lower)
-
-            @pl.when(j < pairs - 1)
-            def _():
-                build(k + 2, j + 1, lower)
-        return 0
-
-    lax.fori_loop(0, pairs, spread, 0)
+            combine(2 * j + (0 if lower else 1), j, lower)
+
+        @pl.when(j == 1)
+        def _():
+            lax.fori_loop(0, sky_tiles, border, 0)
+            halo.start()
+
+        @pl.when(j < pairs - AHEAD)
+        def _():
+            for lower in (True, False):
+                build(2 * (j + AHEAD) + (0 if lower else 1), j + AHEAD, lower)
+        return 0
+
+    lax.fori_loop(1, pairs, spread, 0)
 
     def middle(j, _):
         for lower in (True, False):
@@ -280,6 +300,7 @@
             lax.fori_loop(0, size, one, 0, unroll=2)
             for copy in second_copies(k, j, lower):
                 copy.start()
+            swap(k).wait_send()
         return 0
 
     lax.fori_loop(0, pairs, middle, 0)
@@ -293,6 +314,14 @@
             last_sem.at[0, k], last_sem.at[1, k],
             device_id={"pgroup": partner}, device_id_type=MESH,
         )
+
+    def rows_of(j, lower):
+        sky_block, start = place_of(j, lower)
+        return pl.ds(pl.multiple_of(sky_block * BLOCK + start, ROWS), ROWS)
+
+    def store(k, j, lower, a):
+        rows = rows_of(j, lower)
+        return pltpu.make_async_copy(ready.at[a, rows], out.at[a, rows], out_sem.at[a, k])
 
     def finish(j, _):
         for lower in (True, False):
@@ -301,8 +330,7 @@
                 copy.wait_recv()
             source = second_a if lower else second_b
             count = ny if lower else nx
-            row = (pairs - 1 - j) * BLOCK + (ROWS if lower else 0)
-            rows = pl.ds(pl.multiple_of(row, ROWS), ROWS)
+            rows = rows_of(j, lower)
 
             def summed(s):
                 total = canvas[k, mine(lower) + s]
@@ -314,25 +342,39 @@
                 canvas[k, mine(lower) + (1 - core) * half + s] = summed((1 - core) * half + s)
             last_copy(k, lower).start()
             for s in range(half):
-                out[core, rows, s * LANES : (s + 1) * LANES] = summed(core * half + s)
-        return 0
-
-    lax.fori_loop(0, pairs, finish, 0)
+                ready[core, rows, s * LANES : (s + 1) * LANES] = summed(core * half + s)
+            store(k, j, lower, core).start()
+            for copy in first_copies(k, j, lower):
+                copy.wait_send()
+
+        @pl.when(j >= LAG)
+        def _():
+            receive(j - LAG, 0)
+
+        return 0
 
     def receive(j, _):
         for lower in (True, False):
             k = 2 * j + (0 if lower else 1)
             last_copy(k, lower).wait()
-            row = (pairs - 1 - j) * BLOCK + (ROWS if lower else 0)
-            rows = pl.ds(pl.multiple_of(row, ROWS), ROWS)
+            rows = rows_of(j, lower)
             for s in range(half):
-                out[1 - core, rows, s * LANES : (s + 1) * LANES] = last[k, s]
-            swap(k).wait_send()
-            for copy in first_copies(k, j, lower) + second_copies(k, j, lower):
+                ready[1 - core, rows, s * LANES : (s + 1) * LANES] = last[k, s]
+            store(k, j, lower, 1 - core).start()
+            for copy in second_copies(k, j, lower):
                 copy.wait_send()
         return 0
 
-    lax.fori_loop(0, pairs, receive, 0)
+    lax.fori_loop(0, pairs, finish, 0)
+    lax.fori_loop(pairs - LAG, pairs, receive, 0)
+
+    def stored(j, _):
+        for lower in (True, False):
+            for a in (core, 1 - core):
+                store(2 * j + (0 if lower else 1), j, lower, a).wait()
+        return 0
+
+    lax.fori_loop(0, pairs, stored, 0)
     halo.wait_send()
 
 
@@ -342,7 +384,7 @@
     col_tiles = width // LANES
     sky_tiles = SKY_COLS // LANES
     own = sky_tiles // (ny * nx)
-    pairs = TILE_BLOCKS
+    pairs = TILE_BLOCKS * PER_BLOCK
     chunks = 2 * pairs
     own_cols = SKY_COLS // (2 * ny * nx)
     most = max(nx, ny) - 1
@@ -352,10 +394,9 @@
         functools.partial(kernel, ny, nx, n_tile),
         out_shape=jax.ShapeDtypeStruct((2, TILE_BLOCKS * BLOCK, own_cols), F32),
         in_specs=[pl.BlockSpec(memory_space=pl.ANY)] * 2 + [smem] * 5,
-        out_specs=pl.BlockSpec(memory_space=pltpu.VMEM),
+        out_specs=pl.BlockSpec(memory_space=pl.ANY),
         scratch_shapes=[
-            pltpu.VMEM((points, img_rows, width), F32),
-            pltpu.VMEM((points, img_rows, width), F32),
+            pltpu.VMEM((2, points, img_rows, width), F32),
             pltpu.VMEM((4, BLOCK + 16, LANES), F32),
             pltpu.VMEM((2 * points * blocks * col_tiles + 1, TALL, LANES), F32),
             pltpu.VMEM((2, sky_tiles, 8, LANES), F32),
@@ -368,11 +409,13 @@
             pltpu.VMEM((pairs, ny - 1, own, ROWS, LANES), F32),
             pltpu.VMEM((pairs, nx - 1, own, ROWS, LANES), F32),
             pltpu.VMEM((chunks, own // 2, ROWS, LANES), F32),
+            pltpu.VMEM((2, TILE_BLOCKS * BLOCK, own_cols), F32),
             dma((2, points * blocks)),
             dma((2,)),
             dma((2, chunks)),
             dma((2, chunks, most)),
             dma((2, chunks, most)),
+            dma((2, chunks)),
             dma((2, chunks)),
         ],
         compiler_params=pltpu.CompilerParams(

time: 94.2 us -> 87.7 us (0.931)
  Pallas kernels: 90 us -> 83.5 us
    pallas_call x1, Pallas kernels: 90 us -> 83.5 us  [body(): pl.pallas_call(functools.partial(kernel, ny, nx, n_tile), out_shape=jax.S...]
where the time goes in v2:
time: 87.7 us; the launch traced here: 87.5 us
  Pallas kernels  83.5 us (95%)
  other arithmetic  3.39 us (4%)
    pallas_call x1, Pallas kernels, body(): pl.pallas_call(functools.partial(kernel, ny, nx, n_tile), out_shape=jax.S...  83.5 us
    div x1, other arithmetic, body(): normalised = numer / jnp.maximum(weight, 0.05)  3.39 us

profile of v2, /device:TPU:0, one launch (start us, length us, event | category | flops | bytes accessed | tf_op | source)
XLA Modules:
  0.0 87.5 jit_solution(5869335159458883193)
XLA Ops:
  0.6 83.5 %combine.1 = f32[2,512,512]{2,1,0:T(8,128)} custom-call(f32[2,256,2048]{2,1,0:T(8,128)} %images.1, f32[2,256,2048]{2,1,0:T(8,128)} %beams.1, s32[2]{0:T(128)} %row_block.1, s32[2]{0:T(128)} %col_block.1, s32[2,2]{1,0:T(2,128)} %band.1, f32[2]{0:T(128)} %row_frac.1, f32[2]{0:T(128)} %col_frac.1), custom_call_target="tpu_custom_call" | custom-call | tf_op jit(solution)/shard_map/combine/pallas_call | solution.py:393
  84.1 3.4 %maximum_divide_fusion = (f32[512,512]{1,0:T(8,128)}, f32[512,512]{1,0:T(8,128)}, f32[512,512]{1,0:T(8,128)}) fusion(f32[2,512,512]{2,1,0:T(8,128)} %combine.1), kind=kLoop, calls=%fused_computation | loop fusion | flops 524288 | bytes 5242880 | tf_op jit(solution)/shard_map/div | solution.py:428

commit v3 on v2

--- a/solution.py
+++ b/solution.py
@@ -16,7 +16,7 @@
 ROWS = 32
 PER_BLOCK = BLOCK // (2 * ROWS)
 TALL = BLOCK + 8
-AHEAD = 2
+AHEAD = 1
 LAG = 2
 MESH = pl.DeviceIdType.MESH
 F32 = jnp.float32

time: 87.7 us -> 86.7 us (0.989)
  Pallas kernels: 83.5 us -> 82.5 us
    pallas_call x1, Pallas kernels: 83.5 us -> 82.5 us  [body(): pl.pallas_call(functools.partial(kernel, ny, nx, n_tile), out_shape=jax.S...]
where the time goes in v3:
time: 86.7 us; the launch traced here: 86.5 us
  Pallas kernels  82.5 us (95%)
  other arithmetic  3.39 us (4%)
    pallas_call x1, Pallas kernels, body(): pl.pallas_call(functools.partial(kernel, ny, nx, n_tile), out_shape=jax.S...  82.5 us
    div x1, other arithmetic, body(): normalised = numer / jnp.maximum(weight, 0.05)  3.39 us

profile of v3, /device:TPU:0, one launch (start us, length us, event | category | flops | bytes accessed | tf_op | source)
XLA Modules:
  0.0 86.5 jit_solution(142165005643393953)
XLA Ops:
  0.6 82.5 %combine.1 = f32[2,512,512]{2,1,0:T(8,128)} custom-call(f32[2,256,2048]{2,1,0:T(8,128)} %images.1, f32[2,256,2048]{2,1,0:T(8,128)} %beams.1, s32[2]{0:T(128)} %row_block.1, s32[2]{0:T(128)} %col_block.1, s32[2,2]{1,0:T(2,128)} %band.1, f32[2]{0:T(128)} %row_frac.1, f32[2]{0:T(128)} %col_frac.1), custom_call_target="tpu_custom_call" | custom-call | tf_op jit(solution)/shard_map/combine/pallas_call | solution.py:393
  83.1 3.4 %maximum_divide_fusion = (f32[512,512]{1,0:T(8,128)}, f32[512,512]{1,0:T(8,128)}, f32[512,512]{1,0:T(8,128)}) fusion(f32[2,512,512]{2,1,0:T(8,128)} %combine.1), kind=kLoop, calls=%fused_computation | loop fusion | flops 524288 | bytes 5242880 | tf_op jit(solution)/shard_map/div | solution.py:428
